TPU v7x, 32 devices: a whole 2x2x4 slice. The times are simulated.
32 devices in a mesh: groups: 2 (over y), expert: 4 (over z), tensor: 4 (over x, core).
Axes of the slice: x: 2, y: 2, z: 4, core: 2. Of those that a mesh axis runs over, the one named last changes fastest.
Arguments:
- tokens: bfloat16 [256, 4096], P(('groups', 'expert'), 'tensor'), parts along dimension 0, may hold values from -6 to 6
- expert_ids: int32 [256, 8], P(('groups', 'expert')), parts along dimension 0, may hold values from 0 to 63, all different within a row; in each aligned block of 32 rows (0 to 31, 32 to 63, ...) at most 8 rows name the same one
- gate_fixed: int32 [256, 8], P(('groups', 'expert')), parts along dimension 0, may hold values from 1 to 65535
- w_gate: bfloat16 [64, 4096, 768], P('expert', None, 'tensor'), may hold values from -0.09375 to 0.09375
- w_up: bfloat16 [64, 4096, 768], P('expert', None, 'tensor'), may hold values from -0.09375 to 0.09375
- w_down: bfloat16 [64, 768, 4096], P('expert', 'tensor'), may hold values from -0.21875 to 0.21875
Outputs:
- mixed: bfloat16 [256, 4096], P(('groups', 'expert'), 'tensor'), parts along dimension 0
There are 2 independent parts, one for each index of `groups`. A program takes and returns all parts, laid end to end along the dimension named above; an argument that names none is the same for every part. Nothing has to cross between parts.
Inputs may be any that keep to these rules, and one draw needn't show every extreme that they name: `expert_ids`: each row names 8 different experts. Within the 32 rows of one index of the expert axis no expert is named more than 8 times, and in every draw some expert is named exactly 8 times in some such block.
All inputs are finite; a program needn't handle non-finite values.
Results may differ from a plain program's by a relative error of at most 0.014.
Values may be sent and summed in bfloat16 or wider, within the bound.
A program may use at most 128 MiB of HBM per device.

v0:
```python
import functools

import jax
import jax.numpy as jnp
from jax import lax
from jax.experimental import pallas as pl
from jax.experimental.pallas import tpu as pltpu
from jax.sharding import PartitionSpec as P

CAP = 8


def expert_block(slot_rows, w_gate, w_up, w_down):
    gate_proj = jnp.einsum("gekd,edf->gekf", slot_rows, w_gate, preferred_element_type=jnp.float32)
    up_proj = jnp.einsum("gekd,edf->gekf", slot_rows, w_up, preferred_element_type=jnp.float32)
    hidden = (jax.nn.silu(gate_proj) * up_proj).astype(jnp.bfloat16)
    partial_value = jnp.einsum("gekf,efd->gekd", hidden, w_down, preferred_element_type=jnp.float32)
    summed = lax.psum_scatter(
        partial_value.astype(jnp.bfloat16), "tensor", scatter_dimension=3, tiled=True
    )
    return lax.all_to_all(summed, "expert", split_axis=0, concat_axis=0, tiled=True)


def slotted(tokens, expert_ids, gate_fixed, w_gate, w_up, w_down):
    tok_rows, per_token = expert_ids.shape
    local_experts = w_gate.shape[0]
    devices_e = lax.axis_size("expert")
    experts = local_experts * devices_e
    capacity = CAP
    flat_ids = expert_ids.reshape(-1)
    pick_count = tok_rows * per_token
    onehot = (flat_ids[:, None] == jnp.arange(experts, dtype=jnp.int32)[None, :]).astype(jnp.int32)
    before = jnp.cumsum(onehot, axis=0) - onehot
    slot_rank = jnp.sum(before * onehot, axis=1)
    slot_index = flat_ids * capacity + slot_rank
    owner_row = jnp.arange(pick_count, dtype=jnp.int32) // per_token
    slot_token = jnp.full((experts * capacity,), tok_rows, jnp.int32).at[slot_index].set(owner_row)
    padded = jnp.concatenate([tokens, jnp.zeros((1, tokens.shape[1]), tokens.dtype)], axis=0)
    returned = expert_block(
        lax.all_gather(
            lax.all_to_all(
                padded[slot_token].reshape(devices_e, local_experts, capacity, tokens.shape[1]),
                "expert",
                split_axis=0,
                concat_axis=0,
                tiled=True,
            ),
            "tensor",
            axis=3,
            tiled=True,
        ),
        w_gate,
        w_up,
        w_down,
    )
    flat_returned = returned.reshape(experts * capacity, returned.shape[3])
    picked = flat_returned[slot_index].reshape(tok_rows, per_token, returned.shape[3])
    weights = gate_fixed.astype(jnp.float32)
    gate_share = weights / jnp.sum(weights, axis=1, keepdims=True)
    mixed_out = jnp.einsum("tk,tkf->tf", gate_share, picked.astype(jnp.float32))
    return mixed_out.astype(jnp.bfloat16)


MESH = pl.DeviceIdType.MESH
VMEM_BYTES = 66_000_000
GROUP = 4


def fused_kernel(
    tok_rows, feats, experts, hidden_units, E, T,
    x_ref, ids_ref, gates_ref, wg_ref, wu_ref, wd_ref, out_ref,
    ring, down, tok, ids_all, gates_all, acc, hid_t, hid,
    to_partner, from_partner, to_x, from_x, to_z, from_z, own,
    w_sem, d_sem, own_sem, zt_send, zt_recv, zi_send, zi_recv, t_send, t_recv,
    p_send, p_recv, x_send, x_recv, z_send, z_recv,
):
    g, e, t = lax.axis_index("groups"), lax.axis_index("expert"), lax.axis_index("tensor")
    X = T // 2
    x, c = lax.div(t, 2), lax.rem(t, 2)

    def peer(k):
        half, side = (k // 2, k % 2) if isinstance(k, int) else (lax.div(k, 2), lax.rem(k, 2))
        return lax.rem(x + half, X) * 2 + lax.rem(c + side, 2)

    def mirror(k):
        return (-(k // 2)) % X * 2 + k % 2

    def rows_of(block):
        return pl.ds(pl.multiple_of(block * tok_rows, tok_rows), tok_rows)

    def features_of(k):
        return pl.ds(pl.multiple_of(peer(k) * feats, feats), feats)

    pieces = down_pieces(experts, hidden_units)
    piece_rows = experts * hidden_units // pieces

    def weight_copies(k, i):
        slot = (k % 2) * experts + i
        return [
            pltpu.make_async_copy(
                w.at[i, :, features_of(k)],
                ring.at[slot, pl.ds(part * hidden_units, hidden_units), :],
                w_sem.at[slot, part],
            )
            for part, w in enumerate((wg_ref, wu_ref))
        ]

    def down_copy(k, piece):
        rows = pl.ds(pl.multiple_of(piece * piece_rows, piece_rows), piece_rows)
        return pltpu.make_async_copy(
            wd_ref.at[rows, features_of(k)], down.at[k, rows, :], d_sem.at[k, piece]
        )

    local = [
        pltpu.make_async_copy(x_ref, tok.at[0, rows_of(e), :], own_sem.at[0]),
        pltpu.make_async_copy(ids_ref, ids_all.at[e], own_sem.at[1]),
        pltpu.make_async_copy(gates_ref, gates_all.at[e], own_sem.at[2]),
    ]
    for copy in local:
        copy.start()
    for k in range(2):
        @pl.loop(0, experts)
        def _(i, k=k):
            for copy in weight_copies(k, i):
                copy.start()

    barrier = pltpu.get_barrier_semaphore()
    for d in range(1, E):
        pl.semaphore_signal(barrier, inc=1, device_id=(g, lax.rem(e + d, E), t), device_id_type=MESH)
    for k in range(1, T):
        pl.semaphore_signal(barrier, inc=1, device_id=(g, e, peer(k)), device_id_type=MESH)
    pl.semaphore_wait(barrier, E - 1 + T - 1)

    def remote(src, dst, send, recv, where):
        return pltpu.make_async_remote_copy(
            src_ref=src, dst_ref=dst, send_sem=send, recv_sem=recv, device_id=where, device_id_type=MESH
        )

    for copy in local:
        copy.wait()
    held = tok.at[0, rows_of(e), :]
    sent = []

    def go(*args):
        copy = remote(*args)
        copy.start()
        sent.append(copy)

    def arrived(dst, send, recv):
        remote(dst, dst, send, recv, (g, e, peer(1))).wait_recv()

    def spread(source, d):
        block = lax.rem(e + E - d, E)
        for k in [1] + [2 * dx for dx in range(1, X)]:
            m = mirror(k)
            go(source, tok.at[m, rows_of(block), :], t_send.at[k, d], t_recv.at[m, d], (g, e, peer(k)))

    for d in range(1, E):
        where = (g, lax.rem(e + d, E), t)
        go(held, held, zt_send.at[d], zt_recv.at[d], where)
    spread(held, 0)
    for d in range(1, E):
        where = (g, lax.rem(e + d, E), t)
        go(ids_all.at[e], ids_all.at[e], zi_send.at[0, d], zi_recv.at[0, d], where)
        go(gates_all.at[e], gates_all.at[e], zi_send.at[1, d], zi_recv.at[1, d], where)
    for d in range(1, E):
        landed = tok.at[0, rows_of(lax.rem(e + E - d, E)), :]
        arrived(landed, zt_send.at[d], zt_recv.at[d])
        spread(landed, d)
    def project(k, i):
        for n in range(GROUP):
            for copy in weight_copies(k, i + n):
                copy.wait()
        rows = ring[pl.ds((k % 2) * experts + i, GROUP)].reshape(GROUP * 2 * hidden_units, feats)
        return lax.dot_general(rows, tok[k], (((1,), (1,)), ((), ())), preferred_element_type=jnp.float32)

    for k in range(T):
        if k == 1 or (k > 1 and k % 2 == 0):
            for d in range(E):
                block = lax.rem(e + E - d, E)
                landed = tok.at[k, rows_of(block), :]
                arrived(landed, t_send.at[k, d], t_recv.at[k, d])
                if k > 1:
                    go(landed, tok.at[k + 1, rows_of(block), :], t_send.at[k + 1, d], t_recv.at[k + 1, d], (g, e, peer(1)))
        elif k > 1:
            for d in range(E):
                arrived(tok.at[k, rows_of(lax.rem(e + E - d, E)), :], t_send.at[k, d], t_recv.at[k, d])
        if k == T - 1:
            for d in range(1, E):
                s = lax.rem(e + E - d, E)
                arrived(ids_all.at[s], zi_send.at[0, d], zi_recv.at[0, d])
                arrived(gates_all.at[s], zi_send.at[1, d], zi_recv.at[1, d])
            ids = jnp.concatenate([ids_all[s] for s in range(E)], axis=1)
            gates = jnp.concatenate([gates_all[s] for s in range(E)], axis=1).astype(jnp.float32)
            share = gates / jnp.sum(gates, axis=0, keepdims=True)

        @pl.loop(0, experts // GROUP)
        def _(step, k=k):
            i = step * GROUP
            parts = project(k, i).reshape(GROUP, 2 * hidden_units, -1)
            for n in range(GROUP):
                if k == 0:
                    acc[i + n] = parts[n]
                elif k < T - 1:
                    acc[i + n] += parts[n]
                else:
                    both = acc[i + n] + parts[n]
                    gate, up = both[:hidden_units], both[hidden_units:]
                    weight = jnp.sum(jnp.where(ids == e * experts + i + n, share, 0.0), axis=0, keepdims=True)
                    value = gate / (1.0 + jnp.exp(-gate)) * up * weight
                    start = pl.multiple_of((i + n) * hidden_units, hidden_units)
                    hid_t[pl.ds(start, hidden_units), :] = value
            if k + 2 < T:
                for n in range(GROUP):
                    for copy in weight_copies(k + 2, i + n):
                        copy.start()
            if k == 1:
                for n in range(GROUP * T * pieces // experts):
                    j = step * (GROUP * T * pieces // experts) + n
                    order = lax.div(j, pieces)
                    down_copy((T - 1) - order, lax.rem(j, pieces)).start()

    pair = 2 * hidden_units

    @pl.loop(0, experts // 2)
    def _(i):
        start = pl.multiple_of(i * pair, pair)
        hid[:, pl.ds(start, pair)] = jnp.transpose(hid_t[pl.ds(start, pair), :]).astype(jnp.bfloat16)

    width = 256

    parts_n = feats // width

    def down_part(k, n):
        if n == 0:
            for piece in range(pieces):
                down_copy(k, piece).wait()
        return jnp.dot(
            hid[...], down[k, :, n * width:(n + 1) * width], preferred_element_type=jnp.float32
        )

    def meet_partner(dx, n):
        value = down_part(2 * dx, n)
        arrived(from_partner.at[dx, n], p_send.at[dx, n], p_recv.at[dx, n])
        return value + from_partner[dx, n].astype(jnp.float32)

    for dx in reversed(range(X)):
        for n in range(parts_n + 1):
            if n < parts_n:
                to_partner[dx, n] = down_part(2 * dx + 1, n).astype(jnp.bfloat16)
                go(to_partner.at[dx, n], from_partner.at[dx, n], p_send.at[dx, n], p_recv.at[dx, n], (g, e, peer(1)))
            if n and dx:
                back, m = (X - dx) % X, n - 1
                to_x[dx, m] = meet_partner(dx, m).astype(jnp.bfloat16)
                go(to_x.at[dx, m], from_x.at[back, m], x_send.at[dx, m], x_recv.at[back, m], (g, e, peer(2 * dx)))
            elif n:
                own[n - 1] = meet_partner(0, n - 1)
    for n in range(parts_n):
        for other in range(1, X):
            arrived(from_x.at[other, n], x_send.at[other, n], x_recv.at[other, n])
            own[n] += from_x[other, n].astype(jnp.float32)
        for j in range(1, E):
            to_z[j, n] = own[n, rows_of(lax.rem(e + j, E)), :].astype(jnp.bfloat16)
            go(to_z.at[j, n], from_z.at[j, n], z_send.at[j, n], z_recv.at[j, n], (g, lax.rem(e + j, E), t))
    for n in range(parts_n):
        total = own[n, rows_of(e), :]
        for d in range(1, E):
            arrived(from_z.at[d, n], z_send.at[d, n], z_recv.at[d, n])
            total += from_z[d, n].astype(jnp.float32)
        out_ref[:, n * width:(n + 1) * width] = total.astype(out_ref.dtype)
    for copy in sent:
        copy.wait_send()


def down_pieces(experts, hidden_units):
    return 4 if experts % 4 == 0 and experts * hidden_units % 64 == 0 else 1


def scratch_of(tok_rows, feats, experts, hidden_units, E, T, per_token):
    bf16, f32, X, N = jnp.bfloat16, jnp.float32, T // 2, E * tok_rows
    width, parts_n = 256, feats // 256
    dma = pltpu.SemaphoreType.DMA
    return [
        ((2 * experts, 2 * hidden_units, feats), bf16),
        ((T, experts * hidden_units, feats), bf16),
        ((T, N, feats), bf16),
        ((E, per_token, tok_rows), jnp.int32),
        ((E, per_token, tok_rows), jnp.int32),
        ((experts, 2 * hidden_units, N), f32),
        ((experts * hidden_units, N), f32),
        ((N, experts * hidden_units), bf16),
        ((X, parts_n, N, width), bf16),
        ((X, parts_n, N, width), bf16),
        ((X, parts_n, N, width), bf16),
        ((X, parts_n, N, width), bf16),
        ((E, parts_n, tok_rows, width), bf16),
        ((E, parts_n, tok_rows, width), bf16),
        ((parts_n, N, width), f32),
    ], [
        dma((2 * experts, 2)), dma((T, down_pieces(experts, hidden_units))), dma((3,)),
        dma((E,)), dma((E,)), dma((2, E)), dma((2, E)), dma((T, E)), dma((T, E)),
        dma((X, parts_n)), dma((X, parts_n)), dma((X, parts_n)), dma((X, parts_n)), dma((E, parts_n)), dma((E, parts_n)),
    ]


def fits_fused(sizes):
    tok_rows, feats, experts, hidden_units, E, T, per_token = sizes
    if T % 2 or experts % GROUP or experts % 4 or E * tok_rows % 128 or feats % 256 or tok_rows % 16:
        return False
    if 2 * hidden_units % 128 or hidden_units % 16 or T * 4 % experts:
        return False
    buffers, _ = scratch_of(*sizes)
    size = 0
    for shape, kind in buffers:
        count = jnp.dtype(kind).itemsize
        for length in shape:
            count *= length
        size += count
    return size < VMEM_BYTES - 2_000_000


def on_device(tokens, expert_ids, gate_fixed, w_gate, w_up, w_down):
    (tok_rows, feats), per_token = tokens.shape, expert_ids.shape[1]
    experts, width, hidden_units = w_gate.shape
    E, T = lax.axis_size("expert"), lax.axis_size("tensor")
    sizes = (tok_rows, feats, experts, hidden_units, E, T, per_token)
    if not fits_fused(sizes):
        return slotted(tokens, expert_ids, gate_fixed, w_gate, w_up, w_down)
    buffers, semaphores = scratch_of(*sizes)
    vmem, anywhere = pl.BlockSpec(memory_space=pltpu.VMEM), pl.BlockSpec(memory_space=pl.ANY)
    return pl.pallas_call(
        functools.partial(fused_kernel, *sizes[:6]),
        out_shape=jax.ShapeDtypeStruct(tokens.shape, tokens.dtype),
        in_specs=[anywhere] * 6,
        out_specs=vmem,
        scratch_shapes=[pltpu.VMEM(shape, kind) for shape, kind in buffers] + semaphores,
        compiler_params=pltpu.CompilerParams(
            collective_id=0, has_side_effects=True, vmem_limit_bytes=VMEM_BYTES
        ),
    )(
        tokens,
        expert_ids.T,
        gate_fixed.T,
        jnp.swapaxes(w_gate, 1, 2),
        jnp.swapaxes(w_up, 1, 2),
        w_down.reshape(experts * hidden_units, width),
    )


def solution(mesh):
    placed = (
        P(("groups", "expert"), "tensor"),
        P(("groups", "expert"), None),
        P(("groups", "expert"), None),
        P("expert", None, "tensor"),
        P("expert", None, "tensor"),
        P("expert", "tensor", None),
    )
    return jax.shard_map(
        on_device,
        mesh=mesh,
        in_specs=placed,
        out_specs=P(("groups", "expert"), "tensor"),
        check_vma=False,
    )
```

profile of v0, /device:TPU:0, one launch (start us, length us, event | category | flops | bytes accessed | tf_op | source)
XLA Modules:
  0.0 52.4 jit_solution(12190839959787516674)
XLA Ops:
  0.0 50.9 %shard_map.64 = bf16[32,1024]{1,0:T(8,128)(2,1)} custom-call(bf16[32,1024]{1,0:T(8,128)(2,1)} %x_ref.1, s32[8,32]{1,0:T(8,128)} %bitcast.8, s32[8,32]{1,0:T(8,128)} %bitcast.9, bf16[16,192,4096]{2,1,0:T(8,128)(2,1)} %bitcast.5, bf16[16,192,4096]{2,1,0:T(8,128)(2,1)} %bitcast.6, bf16[3072,4096]{1,0:T(8,128)(2,1)} %bitcast.7), custom_call_target="tpu_custom_call" | custom-call | tf_op jit(solution)/shard_map/pallas_call | solution.py:331
  50.9 1.5 %copy.8 = bf16[32,1024]{1,0:T(8,128)(2,1)} copy(bf16[32,1024]{1,0:T(8,128)(2,1)} %shard_map.64) | data formatting | bytes 131072
where the time goes:
time: 52.5 us; the launch traced here: 52.4 us
  Pallas kernels  50.9 us (97%)
  local copies, waits for them, and re-layouts  1.47 us (3%)
    pallas_call x1, Pallas kernels, on_device(): pl.pallas_call(functools.partial(fused_kernel, *sizes[:6]), out_shape=jax...  50.9 us
    unnamed x1, local copies, waits for them, and re-layouts  1.47 us

commit v1 on v0

v1 whole, which is shorter than its diff:
```python
import functools

import jax
import jax.numpy as jnp
from jax import lax
from jax.experimental import pallas as pl
from jax.experimental.pallas import tpu as pltpu
from jax.sharding import PartitionSpec as P

CAP = 8


def expert_block(slot_rows, w_gate, w_up, w_down):
    gate_proj = jnp.einsum("gekd,edf->gekf", slot_rows, w_gate, preferred_element_type=jnp.float32)
    up_proj = jnp.einsum("gekd,edf->gekf", slot_rows, w_up, preferred_element_type=jnp.float32)
    hidden = (jax.nn.silu(gate_proj) * up_proj).astype(jnp.bfloat16)
    partial_value = jnp.einsum("gekf,efd->gekd", hidden, w_down, preferred_element_type=jnp.float32)
    summed = lax.psum_scatter(
        partial_value.astype(jnp.bfloat16), "tensor", scatter_dimension=3, tiled=True
    )
    return lax.all_to_all(summed, "expert", split_axis=0, concat_axis=0, tiled=True)


def slotted(tokens, expert_ids, gate_fixed, w_gate, w_up, w_down):
    tok_rows, per_token = expert_ids.shape
    local_experts = w_gate.shape[0]
    devices_e = lax.axis_size("expert")
    experts = local_experts * devices_e
    capacity = CAP
    flat_ids = expert_ids.reshape(-1)
    pick_count = tok_rows * per_token
    onehot = (flat_ids[:, None] == jnp.arange(experts, dtype=jnp.int32)[None, :]).astype(jnp.int32)
    before = jnp.cumsum(onehot, axis=0) - onehot
    slot_rank = jnp.sum(before * onehot, axis=1)
    slot_index = flat_ids * capacity + slot_rank
    owner_row = jnp.arange(pick_count, dtype=jnp.int32) // per_token
    slot_token = jnp.full((experts * capacity,), tok_rows, jnp.int32).at[slot_index].set(owner_row)
    padded = jnp.concatenate([tokens, jnp.zeros((1, tokens.shape[1]), tokens.dtype)], axis=0)
    returned = expert_block(
        lax.all_gather(
            lax.all_to_all(
                padded[slot_token].reshape(devices_e, local_experts, capacity, tokens.shape[1]),
                "expert",
                split_axis=0,
                concat_axis=0,
                tiled=True,
            ),
            "tensor",
            axis=3,
            tiled=True,
        ),
        w_gate,
        w_up,
        w_down,
    )
    flat_returned = returned.reshape(experts * capacity, returned.shape[3])
    picked = flat_returned[slot_index].reshape(tok_rows, per_token, returned.shape[3])
    weights = gate_fixed.astype(jnp.float32)
    gate_share = weights / jnp.sum(weights, axis=1, keepdims=True)
    mixed_out = jnp.einsum("tk,tkf->tf", gate_share, picked.astype(jnp.float32))
    return mixed_out.astype(jnp.bfloat16)


MESH = pl.DeviceIdType.MESH
VMEM_BYTES = 67_000_000
LANES = 128
TILE = 256
SUMS = 6
PRE = 18


def fused_kernel(*args):
    def body(*sums):
        fused_body(sums[:SUMS], sums[SUMS:], *args)

    shape = (args[0] * args[4], TILE)
    pl.run_scoped(body, *[pltpu.ACC(q)(shape, jnp.float32) for q in range(2) for _ in range(SUMS)])


def fused_body(
    sums0, sums1, tok_rows, feats, experts, hidden_units, E, T,
    x_ref, ids_ref, gates_ref, wg_ref, wu_ref, wd_ref, out_ref,
    pool, tok, ids_all, gates_all, acc, hid,
    to_partner, from_partner, to_x, from_x, to_z, from_z, own,
    w_sem, own_sem, zt_send, zt_recv, zi_send, zi_recv, t_send, t_recv,
    p_send, p_recv, x_send, x_recv, z_send, z_recv,
):
    g, e, t = lax.axis_index("groups"), lax.axis_index("expert"), lax.axis_index("tensor")
    X = T // 2
    x, c = lax.div(t, 2), lax.rem(t, 2)
    pairs, half = experts // 2, experts // 4
    wide = 2 * hidden_units
    tall = 2 * wide

    def peer(k):
        half_k, side = k // 2, k % 2
        return lax.rem(x + half_k, X) * 2 + lax.rem(c + side, 2)

    def mirror(k):
        return (-(k // 2)) % X * 2 + k % 2

    def rows_of(block):
        return pl.ds(pl.multiple_of(block * tok_rows, tok_rows), tok_rows)

    def features_of(k):
        return pl.ds(pl.multiple_of(peer(k) * feats, feats), feats)

    def fetch(k, p):
        slot = k * pairs + p
        for part, w in enumerate((wg_ref, wu_ref)):
            for j in range(2):
                pltpu.make_async_copy(
                    w.at[2 * p + j, :, features_of(k)],
                    pool.at[slot, pl.ds(part * wide + j * hidden_units, hidden_units), :],
                    w_sem.at[slot],
                ).start()

    def fetched(slot):
        pltpu.make_async_copy(pool.at[slot], pool.at[slot], w_sem.at[slot]).wait()

    down_slot = {T - 1: T * pairs, T - 2: 0, 1: pairs, 0: half}

    def fetch_down(k):
        for q in range(half):
            slot = down_slot[k] + q
            pltpu.make_async_copy(
                wd_ref.at[pl.ds(q * tall, tall), features_of(k)], pool.at[slot], w_sem.at[slot]
            ).start()

    def turn_band(slot, r):
        at = (slot, slice(r * LANES, (r + 1) * LANES))
        band = pool[at]
        pool[at] = jnp.concatenate(
            [jnp.transpose(band[:, f * LANES:(f + 1) * LANES]) for f in range(feats // LANES)], axis=1
        )

    def turn(slot):
        for r in range(tall // LANES):
            turn_band(slot, r)

    def turned(slot, n, f):
        bands = [
            pool[slot, (2 * n + r) * LANES:(2 * n + r + 1) * LANES, f * TILE:(f + 1) * TILE] for r in range(2)
        ]
        return jnp.concatenate(
            [jnp.concatenate([band[:, j * LANES:(j + 1) * LANES] for band in bands], axis=1) for j in range(2)],
            axis=0,
        )

    sums, stage, turn_of = (sums0, sums1), [0, 0], [0, 0]

    def multiply(jobs, lag, side=()):
        side, done, total = list(side), 0, sum(len(steps) for steps, _ in jobs[0])
        begun = len(side)
        waiting = []
        for pair in zip(*jobs):
            used = []
            for q in range(2):
                used.append(sums[q][turn_of[q] % SUMS])
                turn_of[q] += 1
            for s in range(len(pair[0][0])):
                for q in range(2):
                    rows, weights, flip = pair[q][0][s]
                    at = stage[q] % 2
                    stage[q] += 1
                    pltpu.matmul_push_rhs(weights(), staging_register=at, mxu_index=q, transpose=flip)
                    pltpu.matmul_acc_lhs(used[q], rows(), load_staged_rhs=at)
                done += 1
                while side and begun - len(side) < begun * done // total:
                    side.pop(0)()
            waiting.append([(pair[q][1], used[q]) for q in range(2)])
            while len(waiting) > lag:
                for sink, used_sum in waiting.pop(0):
                    sink(pltpu.matmul_pop(used_sum))
        for rest in waiting:
            for sink, used_sum in rest:
                sink(pltpu.matmul_pop(used_sum))

    local = [
        pltpu.make_async_copy(x_ref, tok.at[0, rows_of(e), :], own_sem.at[0]),
        pltpu.make_async_copy(ids_ref, ids_all.at[e], own_sem.at[1]),
        pltpu.make_async_copy(gates_ref, gates_all.at[e], own_sem.at[2]),
    ]
    for copy in local:
        copy.start()
    for k in range(2):
        @pl.loop(0, pairs)
        def _(p, k=k):
            fetch(k, p)

    barrier = pltpu.get_barrier_semaphore()
    for d in range(1, E):
        pl.semaphore_signal(barrier, inc=1, device_id=(g, lax.rem(e + d, E), t), device_id_type=MESH)
    for k in range(1, T):
        pl.semaphore_signal(barrier, inc=1, device_id=(g, e, peer(k)), device_id_type=MESH)

    def turn_range(first, last):
        @pl.loop(first, last)
        def _(slot):
            fetched(slot)
            turn(slot)

    turn_range(0, 2)
    pl.semaphore_wait(barrier, E - 1 + T - 1)

    def remote(src, dst, send, recv, where):
        return pltpu.make_async_remote_copy(
            src_ref=src, dst_ref=dst, send_sem=send, recv_sem=recv, device_id=where, device_id_type=MESH
        )

    for copy in local:
        copy.wait()
    held = tok.at[0, rows_of(e), :]
    sent = []

    def go(*args):
        copy = remote(*args)
        copy.start()
        sent.append(copy)

    def arrived(dst, send, recv):
        remote(dst, dst, send, recv, (g, e, peer(1))).wait_recv()

    def spread(source, d):
        block = lax.rem(e + E - d, E)
        for k in [1] + [2 * dx for dx in range(1, X)]:
            m = mirror(k)
            go(source, tok.at[m, rows_of(block), :], t_send.at[k, d], t_recv.at[m, d], (g, e, peer(k)))

    for d in range(1, E):
        where = (g, lax.rem(e + d, E), t)
        go(held, held, zt_send.at[d], zt_recv.at[d], where)
    spread(held, 0)
    for d in range(1, E):
        where = (g, lax.rem(e + d, E), t)
        go(ids_all.at[e], ids_all.at[e], zi_send.at[0, d], zi_recv.at[0, d], where)
        go(gates_all.at[e], gates_all.at[e], zi_send.at[1, d], zi_recv.at[1, d], where)
    for k in range(2, T):
        @pl.loop(0, pairs)
        def _(p, k=k):
            fetch(k, p)
    fetch_down(T - 1)

    def from_side(k, d):
        landed = tok.at[k, rows_of(lax.rem(e + E - d, E)), :]
        arrived(landed, t_send.at[k, d], t_recv.at[k, d])
        return landed

    def pass_on(d):
        for k in range(2, T, 2):
            block = lax.rem(e + E - d, E)
            go(
                from_side(k, d), tok.at[k + 1, rows_of(block), :],
                t_send.at[k + 1, d], t_recv.at[k + 1, d], (g, e, peer(1)),
            )

    marks = [2] + [PRE - 7 + (PRE - PRE + 7) * (d - 1) // (E - 1) for d in range(1, E)] + [PRE]
    for d in range(1, E):
        turn_range(marks[d - 1], marks[d])
        landed = tok.at[0, rows_of(lax.rem(e + E - d, E)), :]
        arrived(landed, zt_send.at[d], zt_recv.at[d])
        spread(landed, d)
    turn_range(marks[E - 1], PRE)
    for d in range(E):
        from_side(1, d)

    def early(first, last):
        for slot in range(first, last):
            fetched(slot)
        return range(first, last)

    def steps_of(p, n, ks, flip):
        def step(k, f):
            slot = k * pairs + p
            return (
                lambda: tok[k, :, f * TILE:(f + 1) * TILE],
                lambda: pool[slot, n * TILE:(n + 1) * TILE, f * TILE:(f + 1) * TILE] if flip else turned(slot, n, f),
                flip,
            )

        return [step(k, f) for k in ks for f in range(feats // TILE)]

    tiles = tall // TILE

    def sink_of(p, n, first, last):
        def sink(value):
            at = (p, slice(None), slice(n * TILE, (n + 1) * TILE))
            acc[at] = value if first else acc[at] + value
            if last and n == tiles - 1:
                finish(p)

        return sink

    def jobs_of(members, ks, first=False, last=False, flip=False):
        return [
            [
                (steps_of(p, n, ks, flip), sink_of(p, n, first, last))
                for p in members[q::2] for n in range(tiles)
            ]
            for q in range(2)
        ]

    def bands_of(slots):
        return [functools.partial(turn_band, slot, r) for slot in slots for r in range(tall // LANES)]

    low, high = list(range(half)), list(range(half, pairs))
    third, fourth = 2 * pairs, 3 * pairs
    pass_on(0)
    multiply(jobs_of(low, (0, 1), first=True), 1, bands_of(early(PRE, third + half)))
    fetch_down(T - 2)
    fetch_down(1)
    for d in range(1, E):
        pass_on(d)
    multiply(jobs_of(high, (0, 1), first=True), 1, bands_of(early(third + half, fourth)))
    fetch_down(0)
    for d in range(E):
        from_side(T - 1, d)
    for d in range(1, E):
        s = lax.rem(e + E - d, E)
        arrived(ids_all.at[s], zi_send.at[0, d], zi_recv.at[0, d])
        arrived(gates_all.at[s], zi_send.at[1, d], zi_recv.at[1, d])
    ids = jnp.concatenate([ids_all[s] for s in range(E)], axis=1)
    gates = jnp.concatenate([gates_all[s] for s in range(E)], axis=1).astype(jnp.float32)
    share = jnp.transpose(gates / jnp.sum(gates, axis=0, keepdims=True))
    ids = jnp.transpose(ids)
    first_of_pair = lax.broadcasted_iota(jnp.int32, (E * tok_rows, wide), 1) < hidden_units

    def finish(p):
        both = acc[p]
        gate, up = both[:, :wide], both[:, wide:]
        weight = [
            jnp.sum(jnp.where(ids == e * experts + 2 * p + j, share, 0.0), axis=1, keepdims=True)
            for j in range(2)
        ]
        value = gate / (1.0 + jnp.exp(-gate)) * up * jnp.where(first_of_pair, weight[0], weight[1])
        hid[:, p * wide:(p + 1) * wide] = value.astype(jnp.bfloat16)

    multiply(jobs_of(low + high, (2,)), 1, bands_of(early(fourth, fourth + half)))
    late = high[half // 2:]
    some = early(fourth + half, fourth + half + half // 2)
    for p in late:
        fetched(fourth + p)
    plain, flipped = jobs_of(low, (3,), last=True), jobs_of(late, (3,), last=True, flip=True)
    multiply([plain[q] + flipped[q] for q in range(2)], 1, bands_of(some))
    multiply(jobs_of(high[:half // 2], (3,), last=True), 1)

    parts_n = feats // TILE
    def down_jobs(k, n, sinks):
        if n == 0:
            for q in range(half):
                fetched(down_slot[k] + q)

        def step(q, m, f):
            start = m * tall + f * TILE
            return (
                lambda: hid[:, start:start + TILE],
                lambda: pool[
                    down_slot[k] + m, f * TILE:(f + 1) * TILE, (n + q) * TILE:(n + q + 1) * TILE
                ],
                False,
            )

        multiply(
            [[([step(q, m, f) for m in range(half) for f in range(tiles)], sinks(n + q))] for q in range(2)], 0
        )

    def to_side(dx, n):
        def sinks(n):
            def sink(value):
                to_partner[dx, n] = value.astype(jnp.bfloat16)
                go(
                    to_partner.at[dx, n], from_partner.at[dx, n],
                    p_send.at[dx, n], p_recv.at[dx, n], (g, e, peer(1)),
                )

            return sink

        down_jobs(2 * dx + 1, n, sinks)

    def meet_side(dx, n):
        def sinks(n):
            def sink(value):
                arrived(from_partner.at[dx, n], p_send.at[dx, n], p_recv.at[dx, n])
                met = value + from_partner[dx, n].astype(jnp.float32)
                if dx:
                    back = (X - dx) % X
                    to_x[dx, n] = met.astype(jnp.bfloat16)
                    go(
                        to_x.at[dx, n], from_x.at[back, n],
                        x_send.at[dx, n], x_recv.at[back, n], (g, e, peer(2 * dx)),
                    )
                else:
                    own[n] = met

            return sink

        down_jobs(2 * dx, n, sinks)

    for dx in reversed(range(X)):
        for n in range(0, parts_n, 2):
            to_side(dx, n)
        for n in range(0, parts_n, 2):
            meet_side(dx, n)
    for n in range(parts_n):
        for other in range(1, X):
            arrived(from_x.at[other, n], x_send.at[other, n], x_recv.at[other, n])
            own[n] += from_x[other, n].astype(jnp.float32)
        for j in range(1, E):
            to_z[j, n] = own[n, rows_of(lax.rem(e + j, E)), :].astype(jnp.bfloat16)
            go(to_z.at[j, n], from_z.at[j, n], z_send.at[j, n], z_recv.at[j, n], (g, lax.rem(e + j, E), t))
    for n in range(parts_n):
        total = own[n, rows_of(e), :]
        for d in range(1, E):
            arrived(from_z.at[d, n], z_send.at[d, n], z_recv.at[d, n])
            total += from_z[d, n].astype(jnp.float32)
        out_ref[:, n * TILE:(n + 1) * TILE] = total.astype(out_ref.dtype)
    for copy in sent:
        copy.wait_send()


def scratch_of(tok_rows, feats, experts, hidden_units, E, T, per_token):
    bf16, f32, X, N = jnp.bfloat16, jnp.float32, T // 2, E * tok_rows
    parts_n, tall = feats // TILE, 4 * hidden_units
    slots = T * experts // 2 + experts // 4
    dma = pltpu.SemaphoreType.DMA
    return [
        ((slots, tall, feats), bf16),
        ((T, N, feats), bf16),
        ((E, per_token, tok_rows), jnp.int32),
        ((E, per_token, tok_rows), jnp.int32),
        ((experts // 2, N, tall), f32),
        ((N, experts * hidden_units), bf16),
        ((X, parts_n, N, TILE), bf16),
        ((X, parts_n, N, TILE), bf16),
        ((X, parts_n, N, TILE), bf16),
        ((X, parts_n, N, TILE), bf16),
        ((E, parts_n, tok_rows, TILE), bf16),
        ((E, parts_n, tok_rows, TILE), bf16),
        ((parts_n, N, TILE), f32),
    ], [
        dma((slots,)), dma((3,)),
        dma((E,)), dma((E,)), dma((2, E)), dma((2, E)), dma((T, E)), dma((T, E)),
        dma((X, parts_n)), dma((X, parts_n)), dma((X, parts_n)), dma((X, parts_n)), dma((E, parts_n)), dma((E, parts_n)),
    ]


def fits_fused(sizes):
    tok_rows, feats, experts, hidden_units, E, T, per_token = sizes
    if T != 4 or E < 2 or experts != 16 or E * tok_rows != 128 or feats % 512 or tok_rows % 16:
        return False
    if 2 * hidden_units % 128 or hidden_units % 16:
        return False
    buffers, _ = scratch_of(*sizes)
    size = 0
    for shape, kind in buffers:
        count = jnp.dtype(kind).itemsize
        for length in shape:
            count *= length
        size += count
    return size < VMEM_BYTES - 1_000_000


def on_device(tokens, expert_ids, gate_fixed, w_gate, w_up, w_down):
    (tok_rows, feats), per_token = tokens.shape, expert_ids.shape[1]
    experts, width, hidden_units = w_gate.shape
    E, T = lax.axis_size("expert"), lax.axis_size("tensor")
    sizes = (tok_rows, feats, experts, hidden_units, E, T, per_token)
    if not fits_fused(sizes):
        return slotted(tokens, expert_ids, gate_fixed, w_gate, w_up, w_down)
    buffers, semaphores = scratch_of(*sizes)
    vmem, anywhere = pl.BlockSpec(memory_space=pltpu.VMEM), pl.BlockSpec(memory_space=pl.ANY)
    return pl.pallas_call(
        functools.partial(fused_kernel, *sizes[:6]),
        out_shape=jax.ShapeDtypeStruct(tokens.shape, tokens.dtype),
        in_specs=[anywhere] * 6,
        out_specs=vmem,
        scratch_shapes=[pltpu.VMEM(shape, kind) for shape, kind in buffers] + semaphores,
        compiler_params=pltpu.CompilerParams(
            collective_id=0, has_side_effects=True, vmem_limit_bytes=VMEM_BYTES
        ),
    )(
        tokens,
        expert_ids.T,
        gate_fixed.T,
        jnp.swapaxes(w_gate, 1, 2),
        jnp.swapaxes(w_up, 1, 2),
        w_down.reshape(experts * hidden_units, width),
    )


def solution(mesh):
    placed = (
        P(("groups", "expert"), "tensor"),
        P(("groups", "expert"), None),
        P(("groups", "expert"), None),
        P("expert", None, "tensor"),
        P("expert", None, "tensor"),
        P("expert", "tensor", None),
    )
    return jax.shard_map(
        on_device,
        mesh=mesh,
        in_specs=placed,
        out_specs=P(("groups", "expert"), "tensor"),
        check_vma=False,
    )
```

time: 52.5 us -> 44.1 us (0.84)
  Pallas kernels: 50.9 us -> 42.5 us
    pallas_call x1, Pallas kernels: 50.9 us -> 42.5 us  [on_device(): pl.pallas_call(functools.partial(fused_kernel, *sizes[:6]), out_shape=jax...]
where the time goes in v1:
time: 44.1 us; the launch traced here: 44 us
  Pallas kernels  42.5 us (96%)
  local copies, waits for them, and re-layouts  1.47 us (3%)
    pallas_call x1, Pallas kernels, on_device(): pl.pallas_call(functools.partial(fused_kernel, *sizes[:6]), out_shape=jax...  42.5 us
    unnamed x1, local copies, waits for them, and re-layouts  1.47 us

profile of v1, /device:TPU:0, one launch (start us, length us, event | category | flops | bytes accessed | tf_op | source)
XLA Modules:
  0.0 44.0 jit_solution(1660074577451359415)
XLA Ops:
  0.0 42.5 %shard_map.64 = bf16[32,1024]{1,0:T(8,128)(2,1)} custom-call(bf16[32,1024]{1,0:T(8,128)(2,1)} %args_0_.4, s32[8,32]{1,0:T(8,128)} %bitcast.8, s32[8,32]{1,0:T(8,128)} %bitcast.9, bf16[16,192,4096]{2,1,0:T(8,128)(2,1)} %bitcast.5, bf16[16,192,4096]{2,1,0:T(8,128)(2,1)} %bitcast.6, bf16[3072,4096]{1,0:T(8,128)(2,1)} %bitcast.7), custom_call_target="tpu_custom_call" | custom-call | tf_op jit(solution)/shard_map/pallas_call | solution.py:472
  42.5 1.5 %copy.8 = bf16[32,1024]{1,0:T(8,128)(2,1)} copy(bf16[32,1024]{1,0:T(8,128)(2,1)} %shard_map.64) | data formatting | bytes 131072

commit v2 on v1

--- a/solution.py
+++ b/solution.py
@@ -62,29 +62,40 @@
 
 
 MESH = pl.DeviceIdType.MESH
-VMEM_BYTES = 67_000_000
+VMEM_BYTES = 66_500_000
 LANES = 128
 TILE = 256
 SUMS = 6
-PRE = 18
+LAG = 1
+PRE = 16
 
 
 def fused_kernel(*args):
-    def body(*sums):
-        fused_body(sums[:SUMS], sums[SUMS:], *args)
-
-    shape = (args[0] * args[4], TILE)
-    pl.run_scoped(body, *[pltpu.ACC(q)(shape, jnp.float32) for q in range(2) for _ in range(SUMS)])
+    tok_rows, feats, experts, _, E, T = args[:6]
+    shape, parts_n, dma = (tok_rows * E, TILE), feats // TILE, pltpu.SemaphoreType.DMA
+
+    def body(*scoped):
+        fused_body(scoped[:SUMS], scoped[SUMS:2 * SUMS], scoped[2 * SUMS:], *args)
+
+    pl.run_scoped(
+        body, *[pltpu.ACC(q)(shape, jnp.float32) for q in range(2) for _ in range(SUMS)],
+        dma((slots_of(experts, T),)), dma((3,)), dma((E,)), dma((2, E)), dma((T, E)),
+        dma((T // 2, parts_n)), dma((T // 2, parts_n)), dma((E, parts_n)),
+    )
+
+
+def slots_of(experts, T):
+    return T * experts // 2 + experts // 4
 
 
 def fused_body(
-    sums0, sums1, tok_rows, feats, experts, hidden_units, E, T,
+    sums0, sums1, local_sems, tok_rows, feats, experts, hidden_units, E, T,
     x_ref, ids_ref, gates_ref, wg_ref, wu_ref, wd_ref, out_ref,
     pool, tok, ids_all, gates_all, acc, hid,
     to_partner, from_partner, to_x, from_x, to_z, from_z, own,
-    w_sem, own_sem, zt_send, zt_recv, zi_send, zi_recv, t_send, t_recv,
-    p_send, p_recv, x_send, x_recv, z_send, z_recv,
+    zt_recv, zi_recv, t_recv, p_recv, x_recv, z_recv,
 ):
+    w_sem, own_sem, zt_send, zi_send, t_send, p_send, x_send, z_send = local_sems
     g, e, t = lax.axis_index("groups"), lax.axis_index("expert"), lax.axis_index("tensor")
     X = T // 2
     x, c = lax.div(t, 2), lax.rem(t, 2)
@@ -149,16 +160,14 @@
 
     sums, stage, turn_of = (sums0, sums1), [0, 0], [0, 0]
 
-    def multiply(jobs, lag, side=()):
-        side, done, total = list(side), 0, sum(len(steps) for steps, _ in jobs[0])
-        begun = len(side)
+    def multiply(jobs, lag, side=(), pause=None):
+        side, done = list(side), 0
+        total, begun = sum(len(steps) for steps, _ in jobs[0]), len(side)
         waiting = []
-        for pair in zip(*jobs):
-            used = []
-            for q in range(2):
-                used.append(sums[q][turn_of[q] % SUMS])
-                turn_of[q] += 1
-            for s in range(len(pair[0][0])):
+
+        def run(pair, used, steps):
+            nonlocal done
+            for s in steps:
                 for q in range(2):
                     rows, weights, flip = pair[q][0][s]
                     at = stage[q] % 2
@@ -168,13 +177,29 @@
                 done += 1
                 while side and begun - len(side) < begun * done // total:
                     side.pop(0)()
-            waiting.append([(pair[q][1], used[q]) for q in range(2)])
-            while len(waiting) > lag:
+
+        def drain(limit):
+            while len(waiting) > limit:
                 for sink, used_sum in waiting.pop(0):
                     sink(pltpu.matmul_pop(used_sum))
-        for rest in waiting:
-            for sink, used_sum in rest:
-                sink(pltpu.matmul_pop(used_sum))
+
+        pairs_of = list(zip(*jobs))
+        uses = []
+        for _ in pairs_of:
+            uses.append([sums[q][turn_of[q] % SUMS] for q in range(2)])
+            for q in range(2):
+                turn_of[q] += 1
+        cut = 0
+        if pause is not None:
+            cut = len(jobs[0][0][0]) // 2
+            for pair, used in zip(pairs_of, uses):
+                run(pair, used, range(cut))
+            pause()
+        for pair, used in zip(pairs_of, uses):
+            run(pair, used, range(cut, len(pair[0][0])))
+            waiting.append([(pair[q][1], used[q]) for q in range(2)])
+            drain(lag)
+        drain(0)
 
     local = [
         pltpu.make_async_copy(x_ref, tok.at[0, rows_of(e), :], own_sem.at[0]),
@@ -225,16 +250,16 @@
         block = lax.rem(e + E - d, E)
         for k in [1] + [2 * dx for dx in range(1, X)]:
             m = mirror(k)
-            go(source, tok.at[m, rows_of(block), :], t_send.at[k, d], t_recv.at[m, d], (g, e, peer(k)))
+            go(source, tok.at[m, rows_of(block), :], t_send.at[k, d], t_recv.at[m - 1, d], (g, e, peer(k)))
 
     for d in range(1, E):
         where = (g, lax.rem(e + d, E), t)
-        go(held, held, zt_send.at[d], zt_recv.at[d], where)
+        go(held, held, zt_send.at[d], zt_recv.at[d - 1], where)
     spread(held, 0)
     for d in range(1, E):
         where = (g, lax.rem(e + d, E), t)
-        go(ids_all.at[e], ids_all.at[e], zi_send.at[0, d], zi_recv.at[0, d], where)
-        go(gates_all.at[e], gates_all.at[e], zi_send.at[1, d], zi_recv.at[1, d], where)
+        go(ids_all.at[e], ids_all.at[e], zi_send.at[0, d], zi_recv.at[0, d - 1], where)
+        go(gates_all.at[e], gates_all.at[e], zi_send.at[1, d], zi_recv.at[1, d - 1], where)
     for k in range(2, T):
         @pl.loop(0, pairs)
         def _(p, k=k):
@@ -243,7 +268,7 @@
 
     def from_side(k, d):
         landed = tok.at[k, rows_of(lax.rem(e + E - d, E)), :]
-        arrived(landed, t_send.at[k, d], t_recv.at[k, d])
+        arrived(landed, t_send.at[k, d], t_recv.at[k - 1, d])
         return landed
 
     def pass_on(d):
@@ -251,18 +276,17 @@
             block = lax.rem(e + E - d, E)
             go(
                 from_side(k, d), tok.at[k + 1, rows_of(block), :],
-                t_send.at[k + 1, d], t_recv.at[k + 1, d], (g, e, peer(1)),
+                t_send.at[k + 1, d], t_recv.at[k, d], (g, e, peer(1)),
             )
 
-    marks = [2] + [PRE - 7 + (PRE - PRE + 7) * (d - 1) // (E - 1) for d in range(1, E)] + [PRE]
+    marks = [2] + [PRE - 5 + 5 * (d - 1) // (E - 2) for d in range(1, E)]
     for d in range(1, E):
         turn_range(marks[d - 1], marks[d])
+        if d == E - 1:
+            pass_on(0)
         landed = tok.at[0, rows_of(lax.rem(e + E - d, E)), :]
-        arrived(landed, zt_send.at[d], zt_recv.at[d])
+        arrived(landed, zt_send.at[d], zt_recv.at[d - 1])
         spread(landed, d)
-    turn_range(marks[E - 1], PRE)
-    for d in range(E):
-        from_side(1, d)
 
     def early(first, last):
         for slot in range(first, last):
@@ -305,20 +329,24 @@
 
     low, high = list(range(half)), list(range(half, pairs))
     third, fourth = 2 * pairs, 3 * pairs
-    pass_on(0)
-    multiply(jobs_of(low, (0, 1), first=True), 1, bands_of(early(PRE, third + half)))
+
+    def beside():
+        for d in range(E):
+            from_side(1, d)
+        pass_on(1)
+
+    multiply(jobs_of(low, (0, 1), first=True), LAG, bands_of(early(PRE, third + half)), beside)
     fetch_down(T - 2)
     fetch_down(1)
-    for d in range(1, E):
+    pass_on(2)
+    multiply(jobs_of(high, (0, 1), first=True), LAG, bands_of(early(third + half, fourth)))
+    fetch_down(0)
+    for d in range(3, E):
         pass_on(d)
-    multiply(jobs_of(high, (0, 1), first=True), 1, bands_of(early(third + half, fourth)))
-    fetch_down(0)
-    for d in range(E):
-        from_side(T - 1, d)
     for d in range(1, E):
         s = lax.rem(e + E - d, E)
-        arrived(ids_all.at[s], zi_send.at[0, d], zi_recv.at[0, d])
-        arrived(gates_all.at[s], zi_send.at[1, d], zi_recv.at[1, d])
+        arrived(ids_all.at[s], zi_send.at[0, d], zi_recv.at[0, d - 1])
+        arrived(gates_all.at[s], zi_send.at[1, d], zi_recv.at[1, d - 1])
     ids = jnp.concatenate([ids_all[s] for s in range(E)], axis=1)
     gates = jnp.concatenate([gates_all[s] for s in range(E)], axis=1).astype(jnp.float32)
     share = jnp.transpose(gates / jnp.sum(gates, axis=0, keepdims=True))
@@ -335,14 +363,16 @@
         value = gate / (1.0 + jnp.exp(-gate)) * up * jnp.where(first_of_pair, weight[0], weight[1])
         hid[:, p * wide:(p + 1) * wide] = value.astype(jnp.bfloat16)
 
-    multiply(jobs_of(low + high, (2,)), 1, bands_of(early(fourth, fourth + half)))
+    multiply(jobs_of(low + high, (2,)), LAG, bands_of(early(fourth, fourth + half)))
+    for d in range(E):
+        from_side(T - 1, d)
     late = high[half // 2:]
     some = early(fourth + half, fourth + half + half // 2)
     for p in late:
         fetched(fourth + p)
     plain, flipped = jobs_of(low, (3,), last=True), jobs_of(late, (3,), last=True, flip=True)
-    multiply([plain[q] + flipped[q] for q in range(2)], 1, bands_of(some))
-    multiply(jobs_of(high[:half // 2], (3,), last=True), 1)
+    multiply([plain[q] + flipped[q] for q in range(2)], LAG, bands_of(some))
+    multiply(jobs_of(high[:half // 2], (3,), last=True), LAG)
 
     parts_n = feats // TILE
     def down_jobs(k, n, sinks):
@@ -387,7 +417,7 @@
                     to_x[dx, n] = met.astype(jnp.bfloat16)
                     go(
                         to_x.at[dx, n], from_x.at[back, n],
-                        x_send.at[dx, n], x_recv.at[back, n], (g, e, peer(2 * dx)),
+                        x_send.at[dx, n], x_recv.at[back - 1, n], (g, e, peer(2 * dx)),
                     )
                 else:
                     own[n] = met
@@ -403,15 +433,15 @@
             meet_side(dx, n)
     for n in range(parts_n):
         for other in range(1, X):
-            arrived(from_x.at[other, n], x_send.at[other, n], x_recv.at[other, n])
+            arrived(from_x.at[other, n], x_send.at[other, n], x_recv.at[other - 1, n])
             own[n] += from_x[other, n].astype(jnp.float32)
         for j in range(1, E):
             to_z[j, n] = own[n, rows_of(lax.rem(e + j, E)), :].astype(jnp.bfloat16)
-            go(to_z.at[j, n], from_z.at[j, n], z_send.at[j, n], z_recv.at[j, n], (g, lax.rem(e + j, E), t))
+            go(to_z.at[j, n], from_z.at[j, n], z_send.at[j, n], z_recv.at[j - 1, n], (g, lax.rem(e + j, E), t))
     for n in range(parts_n):
         total = own[n, rows_of(e), :]
         for d in range(1, E):
-            arrived(from_z.at[d, n], z_send.at[d, n], z_recv.at[d, n])
+            arrived(from_z.at[d, n], z_send.at[d, n], z_recv.at[d - 1, n])
             total += from_z[d, n].astype(jnp.float32)
         out_ref[:, n * TILE:(n + 1) * TILE] = total.astype(out_ref.dtype)
     for copy in sent:
@@ -421,7 +451,7 @@
 def scratch_of(tok_rows, feats, experts, hidden_units, E, T, per_token):
     bf16, f32, X, N = jnp.bfloat16, jnp.float32, T // 2, E * tok_rows
     parts_n, tall = feats // TILE, 4 * hidden_units
-    slots = T * experts // 2 + experts // 4
+    slots = slots_of(experts, T)
     dma = pltpu.SemaphoreType.DMA
     return [
         ((slots, tall, feats), bf16),
@@ -438,15 +468,13 @@
         ((E, parts_n, tok_rows, TILE), bf16),
         ((parts_n, N, TILE), f32),
     ], [
-        dma((slots,)), dma((3,)),
-        dma((E,)), dma((E,)), dma((2, E)), dma((2, E)), dma((T, E)), dma((T, E)),
-        dma((X, parts_n)), dma((X, parts_n)), dma((X, parts_n)), dma((X, parts_n)), dma((E, parts_n)), dma((E, parts_n)),
+        dma((E - 1,)), dma((2, E - 1)), dma((T - 1, E)), dma((X, parts_n)), dma((X - 1, parts_n)), dma((E - 1, parts_n)),
     ]
 
 
 def fits_fused(sizes):
     tok_rows, feats, experts, hidden_units, E, T, per_token = sizes
-    if T != 4 or E < 2 or experts != 16 or E * tok_rows != 128 or feats % 512 or tok_rows % 16:
+    if T != 4 or E != 4 or experts != 16 or E * tok_rows != 128 or feats % 512 or tok_rows % 16:
         return False
     if 2 * hidden_units % 128 or hidden_units % 16:
         return False
@@ -471,7 +499,7 @@
     vmem, anywhere = pl.BlockSpec(memory_space=pltpu.VMEM), pl.BlockSpec(memory_space=pl.ANY)
     return pl.pallas_call(
         functools.partial(fused_kernel, *sizes[:6]),
-        out_shape=jax.ShapeDtypeStruct(tokens.shape, tokens.dtype),
+        out_shape=pltpu.VMEM(tokens.shape, tokens.dtype),
         in_specs=[anywhere] * 6,
         out_specs=vmem,
         scratch_shapes=[pltpu.VMEM(shape, kind) for shape, kind in buffers] + semaphores,

time: 44.1 us -> 40.4 us (0.916)
  Pallas kernels: 42.5 us -> 39.6 us
  local copies, waits for them, and re-layouts: 1.47 us -> 0.63 us
    pallas_call x1, Pallas kernels: 42.5 us -> 39.6 us  [on_device(): pl.pallas_call(functools.partial(fused_kernel, *sizes[:6]), out_shape=plt...]
    unnamed x1, local copies, waits for them, and re-layouts: 1.47 us -> 0.63 us
where the time goes in v2:
time: 40.4 us; the launch traced here: 40.3 us
  Pallas kernels  39.6 us (98%)
  local copies, waits for them, and re-layouts  0.63 us (2%)
    pallas_call x1, Pallas kernels, on_device(): pl.pallas_call(functools.partial(fused_kernel, *sizes[:6]), out_shape=plt...  39.6 us

profile of v2, /device:TPU:0, one launch (start us, length us, event | category | flops | bytes accessed | tf_op | source)
XLA Modules:
  0.0 40.3 jit_solution(10796951611039408752)
XLA Ops:
  0.0 39.6 %shard_map.64 = bf16[32,1024]{1,0:T(8,128)(2,1)S(1)} custom-call(bf16[32,1024]{1,0:T(8,128)(2,1)} %args_0_.4, s32[8,32]{1,0:T(8,128)} %bitcast.8, s32[8,32]{1,0:T(8,128)} %bitcast.9, bf16[16,192,4096]{2,1,0:T(8,128)(2,1)} %bitcast.5, bf16[16,192,4096]{2,1,0:T(8,128)(2,1)} %bitcast.6, bf16[3072,4096]{1,0:T(8,128)(2,1)} %bitcast.7), custom_call_target="tpu_custom_call" | custom-call | tf_op jit(solution)/shard_map/pallas_call | solution.py:500
  39.6 0.6 %copy.8 = bf16[32,1024]{1,0:T(8,128)(2,1)} copy(bf16[32,1024]{1,0:T(8,128)(2,1)S(1)} %shard_map.64) | data formatting | bytes 131072
